TPU v7x, 256 devices: a whole 4x4x8 slice. The times are simulated.
256 devices in a mesh: section: 4 (over y), seq: 64 (over z, x, core).
Axes of the slice: x: 4, y: 4, z: 8, core: 2. Of those that a mesh axis runs over, the one named last changes fastest.
Arguments:
- patches: bfloat16 [64, 729, 1152], P('seq'), may hold values from -40 to 40
- fc_gain: float32 [4, 1152], P('section'), may hold values from 0.1 to 1.9
- fc_in: bfloat16 [4, 1152, 2176], P('section', 'seq'), may hold values from -0.1875 to 0.1875
- fc_in_bias: float32 [4, 2176], P('section'), may hold values from -3 to 3
- fc_out: bfloat16 [4, 2176, 1152], P('section', None, 'seq'), may hold values from -0.125 to 0.125
- fc_out_bias: float32 [4, 1152], P('section'), may hold values from -3 to 3
- proj_weight: bfloat16 [1152, 3584], P('seq'), may hold values from -0.1875 to 0.1875
- text_embed: bfloat16 [8192, 3584], P('seq'), may hold values from -40 to 40
- frame_start: int32 [64], replicated, may hold values from 0 to 8191, as said below
- frame_count: int32 [64], replicated, may hold values from 1 to 196, as said below
- segment_ids: int32 [8192], replicated, may hold values from 0 to 2, as said below
- norm_gain: float32 [3584], replicated, may hold values from 0.1 to 1.9
- query_weight: bfloat16 [3584, 2048], P(None, 'section'), may hold values from -3 to 3
- query_bias: float32 [2048], P('section'), may hold values from -3 to 3
- key_weight: bfloat16 [3584, 512], P(None, 'section'), may hold values from -1 to 1
- value_weight: bfloat16 [3584, 512], P(None, 'section'), may hold values from -0.09375 to 0.09375
- value_bias: float32 [512], P('section'), may hold values from -3 to 3
Outputs:
- attended: bfloat16 [8192, 2048], P('seq', 'section')
Inputs may be any that keep to these rules, and one draw needn't show every extreme that they name: Frame f keeps its first frame_count[f] pooled tokens and places them at positions frame_start[f] to frame_start[f] + frame_count[f] - 1; frame f begins in shard f, at a position from f * 128 to (f + 1) * 128 - 1; every frame ends before the next one begins, and the last ends by position 8191. The frame of shard 64 / 2 - 1 runs into the next shard. `frame_count`: some frame keeps all 196 tokens. `segment_ids`: segment numbers never fall along the sequence, and each of 0, 1 and 2 occurs.
All inputs are finite; a program needn't handle non-finite values.
Results may differ from a plain program's by a relative error of at most 0.02.
Values may be sent and summed in bfloat16 or wider, within the bound.
No kernel may reach another device: no remote copies, remote signals or barrier semaphores. Data moves between devices by JAX's collectives and lax.ppermute only.
A program may use at most 128 MiB of HBM per device.

v0:
```python
import math
import jax
import jax.numpy as jnp
from jax import lax
from jax.sharding import PartitionSpec as P

GRID = 27
layer_eps = 1e-06
rms_eps = 1e-06
rope_base = 1000000.0
mask_floor = -1e30


def turned_gather(arrays, axis, dims):
    turned = [jnp.moveaxis(a, dim, 0) for a, dim in zip(arrays, dims)]
    both = jnp.concatenate([t.reshape(len(t), -1) for t in turned], axis=1)
    filled, at, finished = (lax.all_gather(both, axis, axis=0, tiled=True), 0, [])
    for t, dim in zip(turned, dims):
        section = filled[:, at : at + t[0].size].reshape(-1, *t.shape[1:])
        finished.append(jnp.moveaxis(section, 0, dim))
        at += t[0].size
    return tuple(finished)


def passed_along(block, axis, distance):
    devices = range(lax.axis_size(axis))
    route = [(i - distance, i) for i in devices if i - distance in devices]
    return lax.ppermute(block, axis, route)


def from_root(x, axis, root):
    return lax.dynamic_index_in_dim(lax.all_gather(x, axis), root, 0, keepdims=False)


def layer_norm(values, scales):
    widened = values.astype(jnp.float32)
    center = widened - jnp.mean(widened, axis=-1, keepdims=True)
    spread = jnp.mean(center * center, axis=-1, keepdims=True)
    return center * lax.rsqrt(spread + layer_eps) * scales


def encoder_layer(values, scales, w_in, b_in, w_out, b_out):
    normed = layer_norm(values, scales).astype(jnp.bfloat16)
    hidden = jax.nn.gelu(
        jnp.dot(normed, w_in, preferred_element_type=jnp.float32) + b_in, approximate=True
    ).astype(jnp.bfloat16)
    summed = (
        values.astype(jnp.float32)
        + jnp.dot(hidden, w_out, preferred_element_type=jnp.float32)
        + b_out
    )
    return summed.astype(jnp.bfloat16)


def pool_frame(encoded):
    channel = encoded.shape[-1]
    grid_side = GRID
    pool_side = (GRID + 1) // 2
    grid_cells = encoded.astype(jnp.float32).reshape(grid_side, grid_side, channel)
    pad_cells = 2 * pool_side - grid_side
    grid_cells = jnp.pad(grid_cells, [(0, pad_cells), (0, pad_cells), (0, 0)])
    totals = grid_cells.reshape(pool_side, 2, pool_side, 2, channel).sum(axis=(1, 3))
    counts = jnp.minimum(2, grid_side - 2 * jnp.arange(pool_side)).astype(jnp.float32)
    cell_area = counts[:, None] * counts[None, :]
    return (totals / cell_area[..., None]).reshape(pool_side * pool_side, channel)


def rotate(values, positions):
    head_dim = values.shape[-1]
    half_dim = head_dim // 2
    inv_rates = jnp.exp(
        jnp.arange(half_dim, dtype=jnp.float32) * (-2.0 * math.log(rope_base) / head_dim)
    )
    angles = positions.astype(jnp.float32)[:, None] * inv_rates[None, :]
    cosine = jnp.cos(angles)[:, None, :]
    sine_part = jnp.sin(angles)[:, None, :]
    first_half = values[..., :half_dim]
    second = values[..., half_dim:]
    return jnp.concatenate(
        [first_half * cosine - second * sine_part, second * cosine + first_half * sine_part],
        axis=-1,
    )


def take_rows(source, offsets, upper_limit):
    is_valid = (offsets >= 0) & (offsets < upper_limit)
    picked = jnp.take(source, jnp.clip(offsets, 0, source.shape[0] - 1), axis=0)
    return (jnp.where(is_valid[:, None], picked, jnp.zeros((), source.dtype)), is_valid)


def attend_block(softmax_state, queries, query_pos, query_seg, key_block, block_start, segment_ids):
    row_top, row_total, row_acc = softmax_state
    head_dim = queries.shape[1]
    key_part = key_block[:, :head_dim]
    value_part = key_block[:, head_dim:]
    scores = lax.dot_general(
        queries, key_part, (((1,), (1,)), ((), ())), preferred_element_type=jnp.float32
    )
    scores = scores * (1.0 / math.sqrt(head_dim))
    key_pos = block_start + jnp.arange(key_block.shape[0], dtype=jnp.int32)
    key_seg = lax.dynamic_slice_in_dim(segment_ids, block_start, key_block.shape[0], 0)
    allowed = (key_pos[None, :] <= query_pos[:, None]) & (key_seg[None, :] == query_seg[:, None])
    masked = jnp.where(allowed, scores, mask_floor)
    new_top = jnp.maximum(row_top, jnp.max(masked, axis=1))
    weights = jnp.where(allowed, jnp.exp(masked - new_top[:, None]), 0.0)
    keep_old = jnp.exp(row_top - new_top)
    row_total = row_total * keep_old + jnp.sum(weights, axis=1)
    row_acc = row_acc * keep_old[:, None] + jnp.dot(
        weights.astype(jnp.bfloat16), value_part, preferred_element_type=jnp.float32
    )
    return (new_top, row_total, row_acc)


def per_device(
    patches,
    fc_gain,
    fc_in,
    fc_in_bias,
    fc_out,
    fc_out_bias,
    proj_weight,
    text_embed,
    frame_start,
    frame_count,
    segment_ids,
    norm_gain,
    query_weight,
    query_bias,
    key_weight,
    value_weight,
    value_bias,
):
    section_count = lax.axis_size("section")
    section_id = lax.axis_index("section")
    shard_count = lax.axis_size("seq")
    shard_id = lax.axis_index("seq")
    shard_rows = text_embed.shape[0]
    model_width = text_embed.shape[1]
    head_size = key_weight.shape[1]
    group_size = query_weight.shape[1] // head_size
    frame_patches = patches[0]
    patch_rows, feature_width = frame_patches.shape
    column_count = model_width // section_count
    proj_block = lax.dynamic_slice_in_dim(proj_weight, section_id * column_count, column_count, 1)
    w_in, w_out, proj_full = turned_gather((fc_in, fc_out, proj_block), "seq", (1, 2, 0))
    w_in = w_in[0]
    w_out = w_out[0]
    layer_gain = fc_gain[0]
    bias_in = fc_in_bias[0]
    bias_out = fc_out_bias[0]
    band_rows = 9
    batch_rows = band_rows * GRID
    batches = GRID // band_rows
    tick_count = batches + section_count - 1
    first_section = section_id == 0
    last_section = section_id == section_count - 1

    def run_tick(tick_index, loop_carry):
        inflow, collected = loop_carry
        feed_rows = lax.dynamic_slice_in_dim(
            frame_patches, jnp.minimum(tick_index, batches - 1) * batch_rows, batch_rows, 0
        )
        result = encoder_layer(
            jnp.where(first_section, feed_rows, inflow), layer_gain, w_in, bias_in, w_out, bias_out
        )
        slot_start = jnp.clip(tick_index - section_count + 1, 0, batches - 1) * batch_rows
        current = lax.dynamic_slice_in_dim(collected, slot_start, batch_rows, 0)
        is_ready = last_section & (tick_index >= section_count - 1)
        collected = lax.dynamic_update_slice_in_dim(
            collected, jnp.where(is_ready, result, current), slot_start, 0
        )
        inflow = passed_along(result, "section", 1)
        return (inflow, collected)

    start_state = (
        jnp.zeros((batch_rows, feature_width), jnp.bfloat16),
        jnp.zeros((patch_rows, feature_width), jnp.bfloat16),
    )
    inflow, collected = lax.fori_loop(0, tick_count, run_tick, start_state)
    pooled = pool_frame(collected).astype(jnp.bfloat16)
    local_slots = jnp.arange(shard_rows, dtype=jnp.int32)
    positions = shard_id * shard_rows + local_slots
    own_start = frame_start[shard_id]
    own_count = frame_count[shard_id]
    previous = jnp.maximum(shard_id - 1, 0)
    prev_offsets = positions - frame_start[previous]
    prev_valid = (shard_id > 0) & (prev_offsets >= 0) & (prev_offsets < frame_count[previous])
    own_rows, own_valid = take_rows(pooled, positions - own_start, own_count)
    sent_rows, sent_valid = take_rows(pooled, positions + shard_rows - own_start, own_count)
    arrived = passed_along(sent_rows, "seq", 1)
    vision = jnp.where(own_valid[:, None], own_rows, arrived)
    vision = from_root(vision, "section", section_count - 1)
    block_cols = jnp.dot(vision, proj_full, preferred_element_type=jnp.float32).astype(jnp.bfloat16)
    text_cols = lax.dynamic_slice_in_dim(text_embed, section_id * column_count, column_count, 1)
    mixed_cols = jnp.where((own_valid | prev_valid)[:, None], block_cols, text_cols)
    inputs = lax.all_gather(mixed_cols, "section", axis=1, tiled=True)
    widened = inputs.astype(jnp.float32)
    normed = (
        widened
        * lax.rsqrt(jnp.mean(widened * widened, axis=1, keepdims=True) + rms_eps)
        * norm_gain
    ).astype(jnp.bfloat16)
    queries = jnp.dot(normed, query_weight, preferred_element_type=jnp.float32) + query_bias
    queries = rotate(queries.reshape(shard_rows, group_size, head_size), positions).astype(
        jnp.bfloat16
    )
    queries = queries.reshape(shard_rows * group_size, head_size)
    key_heads = jnp.dot(normed, key_weight, preferred_element_type=jnp.float32)
    key_heads = rotate(key_heads.reshape(shard_rows, 1, head_size), positions).astype(jnp.bfloat16)
    key_heads = key_heads.reshape(shard_rows, head_size)
    values = (
        jnp.dot(normed, value_weight, preferred_element_type=jnp.float32) + value_bias
    ).astype(jnp.bfloat16)
    stacked = jnp.concatenate([key_heads, values], axis=1)
    query_pos = jnp.repeat(positions, group_size)
    query_seg = jnp.repeat(
        lax.dynamic_slice_in_dim(segment_ids, shard_id * shard_rows, shard_rows, 0), group_size
    )
    query_total = shard_rows * group_size
    blank_state = (
        jnp.full((query_total,), mask_floor, jnp.float32),
        jnp.zeros((query_total,), jnp.float32),
        jnp.zeros((query_total, head_size), jnp.float32),
    )
    half_count = shard_count // 2
    is_lower = shard_id < half_count
    quarter = shard_count // 4
    partner_queries = passed_along(queries, "seq", -half_count)
    partner_id = shard_id + half_count
    partner_pos = jnp.repeat(partner_id * shard_rows + local_slots, group_size)
    partner_seg = jnp.repeat(
        lax.dynamic_slice_in_dim(
            segment_ids, jnp.minimum(partner_id, shard_count - 1) * shard_rows, shard_rows, 0
        ),
        group_size,
    )
    own_low = jnp.where(is_lower, 0, quarter * shard_rows)
    own_high = (shard_id + 1) * shard_rows
    part_high = jnp.where(is_lower, quarter * shard_rows, 0)

    def visit_pair(pair_state, key_block, block_start):
        own_state, other_state = pair_state
        own_state = lax.cond(
            (block_start >= own_low) & (block_start < own_high),
            lambda carried: attend_block(
                carried, queries, query_pos, query_seg, key_block, block_start, segment_ids
            ),
            lambda carried: carried,
            own_state,
        )
        other_state = lax.cond(
            block_start < part_high,
            lambda carried: attend_block(
                carried,
                partner_queries,
                partner_pos,
                partner_seg,
                key_block,
                block_start,
                segment_ids,
            ),
            lambda carried: carried,
            other_state,
        )
        return (own_state, other_state)

    initial = (blank_state, blank_state)
    arrived_rows = lax.all_gather(stacked, "seq", axis=0, tiled=True)
    sub_rows = math.gcd(arrived_rows.shape[0], shard_rows)

    def visit_one(block_index, inner_state):
        key_block = lax.dynamic_slice_in_dim(arrived_rows, block_index * sub_rows, sub_rows, 0)
        return visit_pair(inner_state, key_block, block_index * sub_rows)

    folded = lax.fori_loop(0, arrived_rows.shape[0] // sub_rows, visit_one, initial)
    own_state, other_state = folded
    back_top, back_total, back_acc = passed_along(
        (other_state[0], other_state[1], other_state[2]), "seq", half_count
    )
    back_top = jnp.where(is_lower, mask_floor, back_top)
    back_total = jnp.where(is_lower, 0.0, back_total)
    back_acc = jnp.where(is_lower, 0.0, back_acc)
    own_top, own_total, own_acc = own_state
    row_top = jnp.maximum(own_top, back_top)
    keep_own = jnp.exp(own_top - row_top)
    keep_back = jnp.exp(back_top - row_top)
    row_total = own_total * keep_own + back_total * keep_back
    row_acc = own_acc * keep_own[:, None] + back_acc * keep_back[:, None]
    attended = (row_acc / row_total[:, None]).astype(jnp.bfloat16)
    return attended.reshape(shard_rows, group_size * head_size)


def solution(mesh):
    return jax.shard_map(
        per_device,
        mesh=mesh,
        in_specs=(
            P("seq", None, None),
            P("section", None),
            P("section", "seq", None),
            P("section", None),
            P("section", None, "seq"),
            P("section", None),
            P("seq", None),
            P("seq", None),
            P(),
            P(),
            P(),
            P(),
            P(None, "section"),
            P("section"),
            P(None, "section"),
            P(None, "section"),
            P("section"),
        ),
        out_specs=P("seq", "section"),
        check_vma=False,
    )
```

profile of v0, /device:TPU:231, one launch (start us, length us, event | category | flops | bytes accessed | tf_op | source)
XLA Modules:
  0.0 614.5 jit_solution(5960631140011287223)
XLA Ops:
  13.4 91.2 %all-gather.10.cloned.1.call-done = bf16[64,18,5248]{2,1,0:T(8,128)(2,1)} async-done(((bf16[1,18,5248]{2,1,0:T(8,128)(2,1)}), bf16[64,18,5248]{2,1,0:T(8,128)(2,1)}) %all-gather.10.cloned.1.call-update) | async-done | bytes 12091408 | tf_op jit(solution)/shard_map/all_gather | solution.py:17
  104.6 17.1 %reshape.296 = bf16[1152,5248]{1,0:T(8,128)(2,1)} reshape(bf16[64,18,5248]{2,1,0:T(8,128)(2,1)} %all-gather.10.cloned.1.call-done) | data formatting | bytes 24182784
  121.7 8.4 %slice_bitcast_fusion = (bf16[2176,1152]{0,1:T(8,128)(2,1)}, bf16[1152,2176]{1,0:T(8,128)(2,1)}) fusion(bf16[1152,5248]{1,0:T(8,128)(2,1)} %reshape.296), kind=kLoop, calls=%fused_computation.76 | loop fusion | bytes 20054016 | tf_op jit(solution)/shard_map/squeeze | solution.py:147
  130.1 8.5 %copy.23 = bf16[2176,1152]{1,0:T(8,128)(2,1)} copy(bf16[2176,1152]{0,1:T(8,128)(2,1)} %get-tuple-element.956) | data formatting | bytes 10027008 | tf_op jit(solution)/shard_map/while | solution.py:179
  140.0 138.9 %while.43 = (s32[]{:T(128)}, bf16[243,1152]{1,0:T(8,128)(2,1)S(1)}, bf16[729,1152]{1,0:T(8,128)(2,1)}, pred[]{:T(512)}, bf16[729,1152]{1,0:T(8,128)(2,1)}, /*ind...) while((s32[]{:T(128)}, bf16[243,1152]{1,0:T(8,128)(2,1)S(1)}, ...), condition=%wide.region_3.4_spmd, body=%wide.region_0.3_spmd.sunk | while | flops 2446610432 | bytes 18521884 | solution.py:179
  141.8 7.5 %dynamic-slice_select_fusion.4 = (bf16[243,1152]{1,0:T(8,128)(2,1)S(1)}, bf16[243,1152]{1,0:T(8,128)(2,1)S(1)}) fusion(bf16[729,1152]{1,0:T(8,128)(2,1)} %get-tuple-element.1202, s32[]{:T(128)S(6)} %select_n.249, pred[]{:T(512)S(6)} %and.105, f32[1152]{0:T(1024)S(1)} %reduce.8, bf16[2176,1152]{1,0:T(8,128)(2,1)} %get-tuple-element.1227, ...), kind=kOutput, calls=%fused_computation.65.clone.1 | convolution fusion | flops 2444650496 | bytes 12880133 | tf_op jit(solution)/shard_map/while/body/eval_jaxpr/dot_general | solution.py:49
  156.0 8.5 %collective-permute-done = bf16[243,1152]{1,0:T(8,128)(2,1)S(1)} collective-permute-done((bf16[243,1152]{1,0:T(8,128)(2,1)S(1)}, bf16[243,1152]{1,0:T(8,128)(2,1)S(1)}, u32[]{:S(2)}, u32[]{:S(2)}) %collective-permute-start) | collective-permute-done | bytes 559904 | tf_op jit(solution)/shard_map/while/body/eval_jaxpr/ppermute | solution.py:28
  166.3 7.5 %dynamic-slice_select_fusion.4 = (bf16[243,1152]{1,0:T(8,128)(2,1)S(1)}, bf16[243,1152]{1,0:T(8,128)(2,1)S(1)}) fusion(bf16[729,1152]{1,0:T(8,128)(2,1)} %get-tuple-element.1202, s32[]{:T(128)S(6)} %select_n.249, pred[]{:T(512)S(6)} %and.105, f32[1152]{0:T(1024)S(1)} %reduce.8, bf16[2176,1152]{1,0:T(8,128)(2,1)} %get-tuple-element.1227, ...), kind=kOutput, calls=%fused_computation.65.clone.1 | convolution fusion | flops 2444650496 | bytes 12880133 | tf_op jit(solution)/shard_map/while/body/eval_jaxpr/dot_general | solution.py:49
  181.4 7.7 %collective-permute-done = bf16[243,1152]{1,0:T(8,128)(2,1)S(1)} collective-permute-done((bf16[243,1152]{1,0:T(8,128)(2,1)S(1)}, bf16[243,1152]{1,0:T(8,128)(2,1)S(1)}, u32[]{:S(2)}, u32[]{:S(2)}) %collective-permute-start) | collective-permute-done | bytes 559904 | tf_op jit(solution)/shard_map/while/body/eval_jaxpr/ppermute | solution.py:28
  190.9 7.5 %dynamic-slice_select_fusion.4 = (bf16[243,1152]{1,0:T(8,128)(2,1)S(1)}, bf16[243,1152]{1,0:T(8,128)(2,1)S(1)}) fusion(bf16[729,1152]{1,0:T(8,128)(2,1)} %get-tuple-element.1202, s32[]{:T(128)S(6)} %select_n.249, pred[]{:T(512)S(6)} %and.105, f32[1152]{0:T(1024)S(1)} %reduce.8, bf16[2176,1152]{1,0:T(8,128)(2,1)} %get-tuple-element.1227, ...), kind=kOutput, calls=%fused_computation.65.clone.1 | convolution fusion | flops 2444650496 | bytes 12880133 | tf_op jit(solution)/shard_map/while/body/eval_jaxpr/dot_general | solution.py:49
  206.0 6.8 %collective-permute-done = bf16[243,1152]{1,0:T(8,128)(2,1)S(1)} collective-permute-done((bf16[243,1152]{1,0:T(8,128)(2,1)S(1)}, bf16[243,1152]{1,0:T(8,128)(2,1)S(1)}, u32[]{:S(2)}, u32[]{:S(2)}) %collective-permute-start) | collective-permute-done | bytes 559904 | tf_op jit(solution)/shard_map/while/body/eval_jaxpr/ppermute | solution.py:28
  214.6 7.5 %dynamic-slice_select_fusion.4 = (bf16[243,1152]{1,0:T(8,128)(2,1)S(1)}, bf16[243,1152]{1,0:T(8,128)(2,1)S(1)}) fusion(bf16[729,1152]{1,0:T(8,128)(2,1)} %get-tuple-element.1202, s32[]{:T(128)S(6)} %select_n.249, pred[]{:T(512)S(6)} %and.105, f32[1152]{0:T(1024)S(1)} %reduce.8, bf16[2176,1152]{1,0:T(8,128)(2,1)} %get-tuple-element.1227, ...), kind=kOutput, calls=%fused_computation.65.clone.1 | convolution fusion | flops 2444650496 | bytes 12880133 | tf_op jit(solution)/shard_map/while/body/eval_jaxpr/dot_general | solution.py:49
  229.8 6.0 collective-permute-done
  237.5 7.5 %dynamic-slice_select_fusion.4 = (bf16[243,1152]{1,0:T(8,128)(2,1)S(1)}, bf16[243,1152]{1,0:T(8,128)(2,1)S(1)}) fusion(bf16[729,1152]{1,0:T(8,128)(2,1)} %get-tuple-element.1202, s32[]{:T(128)S(6)} %select_n.249, pred[]{:T(512)S(6)} %and.105, f32[1152]{0:T(1024)S(1)} %reduce.8, bf16[2176,1152]{1,0:T(8,128)(2,1)} %get-tuple-element.1227, ...), kind=kOutput, calls=%fused_computation.65.clone.1 | convolution fusion | flops 2444650496 | bytes 12880133 | tf_op jit(solution)/shard_map/while/body/eval_jaxpr/dot_general | solution.py:49
  252.7 5.1 collective-permute-done
  259.6 7.5 %dynamic-slice_select_fusion.4 = (bf16[243,1152]{1,0:T(8,128)(2,1)S(1)}, bf16[243,1152]{1,0:T(8,128)(2,1)S(1)}) fusion(bf16[729,1152]{1,0:T(8,128)(2,1)} %get-tuple-element.1202, s32[]{:T(128)S(6)} %select_n.249, pred[]{:T(512)S(6)} %and.105, f32[1152]{0:T(1024)S(1)} %reduce.8, bf16[2176,1152]{1,0:T(8,128)(2,1)} %get-tuple-element.1227, ...), kind=kOutput, calls=%fused_computation.65.clone.1 | convolution fusion | flops 2444650496 | bytes 12880133 | tf_op jit(solution)/shard_map/while/body/eval_jaxpr/dot_general | solution.py:49
  283.8 5.5 reshape.273
  289.3 4.5 reduce_sum.76
  304.7 33.4 %all-gather.8.cloned.1.call-done = bf16[512,1152]{1,0:T(8,128)(2,1)} async-done(((bf16[128,1152]{1,0:T(8,128)(2,1)}), bf16[512,1152]{1,0:T(8,128)(2,1)}) %all-gather.8.cloned.1.call-update) | async-done | bytes 1179664 | tf_op jit(solution)/shard_map/all_gather | solution.py:32
  340.3 12.5 %all_gather.18 = bf16[128,3584]{1,0:T(8,128)(2,1)S(1)} all-gather(bf16[128,896]{1,0:T(8,128)(2,1)S(1)} %fusion.69), channel_id=1, replica_groups=mesh['section'=4,'seq'=64] {'section'}, dimensions={1}, use_global_device_ids=true | all-gather | bytes 1146880 | tf_op jit(solution)/shard_map/all_gather | solution.py:196
  358.7 4.5 collective-permute-start.2
  365.2 70.4 %all-gather.6.cloned.1.call-done = bf16[8192,256]{0,1:T(8,128)(2,1)} async-done(((bf16[128,256]{0,1:T(8,128)(2,1)}), bf16[8192,256]{0,1:T(8,128)(2,1)}) %all-gather.6.cloned.1.call-update) | async-done | bytes 4194320 | tf_op jit(solution)/shard_map/all_gather | solution.py:268
  435.7 158.5 %while.44 = (s32[]{:T(128)}, f32[512]{0:T(512)S(1)}, f32[512]{0:T(512)S(1)}, f32[512,128]{1,0:T(8,128)S(1)}, f32[512]{0:T(512)S(1)}, /*index=5*/f32[512]{0:T(512...) while((s32[]{:T(128)}, f32[512]{0:T(512)S(1)}, ...), condition=%wide.region_15.17_spmd.clone, body=%wide.region_6.16_spmd.clone.sunk | while | flops 69732624 | bytes 3403379 | solution.py:275
  598.1 8.8 %collective-permute-done.3 = f32[512]{0:T(512)S(1)} collective-permute-done((f32[512]{0:T(512)S(1)}, f32[512]{0:T(512)S(1)}, u32[]{:S(2)}, u32[]{:S(2)}) %collective-permute-start.3) | collective-permute-done | bytes 2080 | tf_op jit(solution)/shard_map/ppermute | solution.py:28
  (967 shorter events, 341.5 us)
Async XLA Ops:
  6.5 346.5 %copy-start = (bf16[3584,128]{1,0:T(8,128)(2,1)S(1)}, bf16[3584,128]{1,0:T(8,128)(2,1)}, u32[]{:S(2)}) copy-start(bf16[3584,128]{1,0:T(8,128)(2,1)} %param.41) | copy-start | bytes 2752516
  6.5 98.1 %all-gather.10.cloned.1.call-start = ((), (), s32[]{:S(2)}) async-start(), calls=%async_computation.2 | async-start | bytes 16373760 | tf_op jit(solution)/shard_map/all_gather | solution.py:17
  9.1 329.0 %all-gather.8.cloned.1.call-start = ((), (), s32[]{:S(2)}) async-start(), calls=%async_computation.1 | async-start | bytes 1474560 | tf_op jit(solution)/shard_map/all_gather | solution.py:32
  138.6 1.4 copy-start.1
  138.6 1.4 copy-start.2
  138.6 1.4 copy-start.3
  149.4 15.1 %collective-permute-start = (bf16[243,1152]{1,0:T(8,128)(2,1)S(1)}, bf16[243,1152]{1,0:T(8,128)(2,1)S(1)}, u32[]{:S(2)}, u32[]{:S(2)}) collective-permute-start(bf16[243,1152]{1,0:T(8,128)(2,1)S(1)} %get-tuple-element.1143), channel_id=1, source_target_pairs={{0,64},{64,128},{128,192},{1,65},{65,129},{129,193},{2,66},{66,130... | collective-permute-start | bytes 1679624 | tf_op jit(solution)/shard_map/while/body/eval_jaxpr/ppermute | solution.py:28
  173.8 15.3 %collective-permute-start = (bf16[243,1152]{1,0:T(8,128)(2,1)S(1)}, bf16[243,1152]{1,0:T(8,128)(2,1)S(1)}, u32[]{:S(2)}, u32[]{:S(2)}) collective-permute-start(bf16[243,1152]{1,0:T(8,128)(2,1)S(1)} %get-tuple-element.1143), channel_id=1, source_target_pairs={{0,64},{64,128},{128,192},{1,65},{65,129},{129,193},{2,66},{66,130... | collective-permute-start | bytes 1679624 | tf_op jit(solution)/shard_map/while/body/eval_jaxpr/ppermute | solution.py:28
  198.4 14.4 %collective-permute-start = (bf16[243,1152]{1,0:T(8,128)(2,1)S(1)}, bf16[243,1152]{1,0:T(8,128)(2,1)S(1)}, u32[]{:S(2)}, u32[]{:S(2)}) collective-permute-start(bf16[243,1152]{1,0:T(8,128)(2,1)S(1)} %get-tuple-element.1143), channel_id=1, source_target_pairs={{0,64},{64,128},{128,192},{1,65},{65,129},{129,193},{2,66},{66,130... | collective-permute-start | bytes 1679624 | tf_op jit(solution)/shard_map/while/body/eval_jaxpr/ppermute | solution.py:28
  222.2 13.5 %collective-permute-start = (bf16[243,1152]{1,0:T(8,128)(2,1)S(1)}, bf16[243,1152]{1,0:T(8,128)(2,1)S(1)}, u32[]{:S(2)}, u32[]{:S(2)}) collective-permute-start(bf16[243,1152]{1,0:T(8,128)(2,1)S(1)} %get-tuple-element.1143), channel_id=1, source_target_pairs={{0,64},{64,128},{128,192},{1,65},{65,129},{129,193},{2,66},{66,130... | collective-permute-start | bytes 1679624 | tf_op jit(solution)/shard_map/while/body/eval_jaxpr/ppermute | solution.py:28
  245.1 12.7 %collective-permute-start = (bf16[243,1152]{1,0:T(8,128)(2,1)S(1)}, bf16[243,1152]{1,0:T(8,128)(2,1)S(1)}, u32[]{:S(2)}, u32[]{:S(2)}) collective-permute-start(bf16[243,1152]{1,0:T(8,128)(2,1)S(1)} %get-tuple-element.1143), channel_id=1, source_target_pairs={{0,64},{64,128},{128,192},{1,65},{65,129},{129,193},{2,66},{66,130... | collective-permute-start | bytes 1679624 | tf_op jit(solution)/shard_map/while/body/eval_jaxpr/ppermute | solution.py:28
  267.1 11.8 %collective-permute-start = (bf16[243,1152]{1,0:T(8,128)(2,1)S(1)}, bf16[243,1152]{1,0:T(8,128)(2,1)S(1)}, u32[]{:S(2)}, u32[]{:S(2)}) collective-permute-start(bf16[243,1152]{1,0:T(8,128)(2,1)S(1)} %get-tuple-element.1143), channel_id=1, source_target_pairs={{0,64},{64,128},{128,192},{1,65},{65,129},{129,193},{2,66},{66,130... | collective-permute-start | bytes 1679624 | tf_op jit(solution)/shard_map/while/body/eval_jaxpr/ppermute | solution.py:28
  295.1 8.4 %collective-permute-start.1 = (bf16[128,1152]{1,0:T(8,128)(2,1)S(1)}, bf16[128,1152]{1,0:T(8,128)(2,1)S(1)}, u32[]{:S(2)}, u32[]{:S(2)}) collective-permute-start(bf16[128,1152]{1,0:T(8,128)(2,1)S(1)} %select_select_fusion), channel_id=1, source_target_pairs={{0,1},{1,2},{2,3},{3,4},{4,5},{5,6},{6,7},{7,8},{8,9},{9,10},{10,1... | collective-permute-start | bytes 884744 | tf_op jit(solution)/shard_map/ppermute | solution.py:28
  304.4 131.2 %all-gather.6.cloned.1.call-start = ((), (), s32[]{:S(2)}) async-start(), calls=%async_computation | async-start | bytes 4259840 | tf_op jit(solution)/shard_map/all_gather | solution.py:268
  338.1 15.0 %copy-start.5 = (f32[3584]{0:T(1024)S(1)}, f32[3584]{0:T(1024)}, u32[]{:S(2)}) copy-start(f32[3584]{0:T(1024)} %param.38) | copy-start | bytes 43012
  340.2 13.4 %copy-start.4 = (bf16[3584,128]{1,0:T(8,128)(2,1)S(1)}, bf16[3584,128]{1,0:T(8,128)(2,1)}, u32[]{:S(2)}) copy-start(bf16[3584,128]{1,0:T(8,128)(2,1)} %param.42) | copy-start | bytes 2752516
  340.3 13.4 %copy-start.7 = (f32[128]{0:T(128)S(1)}, f32[128]{0:T(128)}, u32[]{:S(2)}) copy-start(f32[128]{0:T(128)} %param.43) | copy-start | bytes 1540
  353.1 2.4 copy-start.6
  358.7 6.5 %collective-permute-start.2 = (bf16[512,128]{1,0:T(8,128)(2,1)S(1)}, bf16[512,128]{1,0:T(8,128)(2,1)S(1)}, u32[]{:S(2)}, u32[]{:S(2)}) collective-permute-start(bf16[512,128]{1,0:T(8,128)(2,1)S(1)} %pad_maximum_fusion), channel_id=1, source_target_pairs={{32,0},{33,1},{34,2},{35,3},{36,4},{37,5},{38,6},{39,7},{40,8},{41... | collective-permute-start | bytes 393224 | tf_op jit(solution)/shard_map/ppermute | solution.py:28
  594.2 12.8 %collective-permute-start.4 = (f32[512,128]{1,0:T(8,128)S(1)}, f32[512,128]{1,0:T(8,128)S(1)}, u32[]{:S(2)}, u32[]{:S(2)}) collective-permute-start(f32[512,128]{1,0:T(8,128)S(1)} %get-tuple-element.732), channel_id=1, source_target_pairs={{0,32},{1,33},{2,34},{3,35},{4,36},{5,37},{6,38},{7,39},{8,40},{9,... | collective-permute-start | bytes 786440 | tf_op jit(solution)/shard_map/ppermute | solution.py:28
  595.5 11.4 %collective-permute-start.3 = (f32[512]{0:T(512)S(1)}, f32[512]{0:T(512)S(1)}, u32[]{:S(2)}, u32[]{:S(2)}) collective-permute-start(f32[512]{0:T(512)S(1)} %get-tuple-element.731), channel_id=1, source_target_pairs={{0,32},{1,33},{2,34},{3,35},{4,36},{5,37},{6,38},{7,39},{8,40},{9,... | collective-permute-start | bytes 6152 | tf_op jit(solution)/shard_map/ppermute | solution.py:28
  596.8 10.1 %collective-permute-start.5 = (f32[512]{0:T(512)S(1)}, f32[512]{0:T(512)S(1)}, u32[]{:S(2)}, u32[]{:S(2)}) collective-permute-start(f32[512]{0:T(512)S(1)} %get-tuple-element.734), channel_id=1, source_target_pairs={{0,32},{1,33},{2,34},{3,35},{4,36},{5,37},{6,38},{7,39},{8,40},{9,... | collective-permute-start | bytes 6152 | tf_op jit(solution)/shard_map/ppermute | solution.py:28
Sparse Core Ops, SparseCore 0:
  10.1 94.4 all-gather.9
  304.5 33.4 all-gather.7
  355.3 80.2 all-gather.5
where the time goes:
time: 621 us; the launch traced here: 615 us
  waiting for transfers between devices  246 us (40%)
  local copies, waits for them, and re-layouts  188 us (30%)
  matrix products  78.1 us (13%)
  other arithmetic  34.1 us (5%)
  starting transfers between devices  33.8 us (5%)
  between operations  13.5 us (2%)
  blocking collectives  12.5 us (2%)
  loops' own time  8.41 us (1%)
    all_gather x1, waiting for transfers between devices, turned_gather(): lax.all_gather(both, axis, axis=0, tiled=True)  91.2 us
    all_gather x1, waiting for transfers between devices, per_device(): arrived_rows = lax.all_gather(stacked, 'seq', axis=0, tiled=True)  70.4 us
    dynamic_slice x128, local copies, waits for them, and re-layouts, visit_one(): lax.dynamic_slice_in_dim(arrived_rows, block_index * sub_rows, sub_rows, 0)  61.2 us
    ppermute x11, waiting for transfers between devices, passed_along(): return lax.ppermute(block, axis, route)  51.2 us
    dot_general x6, matrix products, encoder_layer(): jnp.dot(hidden, w_out, preferred_element_type=jnp.float32)  45.1 us
    dynamic_slice x48, local copies, waits for them, and re-layouts, attend_block(): lax.dynamic_slice_in_dim(segment_ids, block_start, key_block.shape[0], 0)  36.7 us
    ppermute x11, starting transfers between devices, passed_along(): return lax.ppermute(block, axis, route)  33.6 us
    all_gather x1, waiting for transfers between devices, from_root(): lax.all_gather(x, axis)  33.4 us
  transfers between devices with their start and end apart: 14, of which 12 were waited for; matrix products, arithmetic and copies ran while one was open for 5% of the time, Pallas kernels for 0%

commit v1 on v0

--- a/solution.py
+++ b/solution.py
@@ -11,10 +11,18 @@
 mask_floor = -1e30
 
 
+def fit_the_sheets(sample, along_axis):
+    all_rows = lax.axis_size(along_axis)
+    e_next = jnp.stack([sample] * all_rows)
+    moved = lax.all_to_all(e_next, along_axis, 0, 0)
+    b_next = jnp.concatenate(moved, 0)
+    return b_next
+
+
 def turned_gather(arrays, axis, dims):
     turned = [jnp.moveaxis(a, dim, 0) for a, dim in zip(arrays, dims)]
     both = jnp.concatenate([t.reshape(len(t), -1) for t in turned], axis=1)
-    filled, at, finished = (lax.all_gather(both, axis, axis=0, tiled=True), 0, [])
+    filled, at, finished = (fit_the_sheets(both, axis), 0, [])
     for t, dim in zip(turned, dims):
         section = filled[:, at : at + t[0].size].reshape(-1, *t.shape[1:])
         finished.append(jnp.moveaxis(section, 0, dim))

time: 621 us -> 891 us (1.43)
  waiting for transfers between devices: 246 us -> 503 us
  starting transfers between devices: 33.8 us -> 43.4 us
    all_to_all x0 -> x1, waiting for transfers between devices: none -> 343 us  [fit_the_sheets(): moved = lax.all_to_all(e_next, along_axis, 0, 0)]
    all_gather x1 -> x0, waiting for transfers between devices: 91.2 us -> none  [turned_gather(): lax.all_gather(both, axis, axis=0, tiled=True)]
    reshape x0 -> x1, local copies, waits for them, and re-layouts: none -> 17.1 us  [fit_the_sheets(): b_next = jnp.concatenate(moved, 0)]
    unnamed x17 -> x20, local copies, waits for them, and re-layouts: 17.1 us -> 0.05 us
    all_to_all x0 -> x1, starting transfers between devices: none -> 9.66 us  [fit_the_sheets(): moved = lax.all_to_all(e_next, along_axis, 0, 0)]
  transfers between devices with their start and end apart: 14 -> 14, of which waited for: 12 -> 12; matrix products, arithmetic and copies ran while one was open for 5% -> 4% of each run, Pallas kernels for 0% -> 0%
where the time goes in v1:
time: 891 us; the launch traced here: 885 us
  waiting for transfers between devices  503 us (56%)
  local copies, waits for them, and re-layouts  192 us (22%)
  matrix products  78.2 us (9%)
  starting transfers between devices  43.4 us (5%)
  other arithmetic  33.5 us (4%)
  between operations  13.8 us (2%)
  blocking collectives  12.7 us (1%)
    all_to_all x1, waiting for transfers between devices, fit_the_sheets(): moved = lax.all_to_all(e_next, along_axis, 0, 0)  343 us
    all_gather x1, waiting for transfers between devices, per_device(): arrived_rows = lax.all_gather(stacked, 'seq', axis=0, tiled=True)  70.4 us
    dynamic_slice x128, local copies, waits for them, and re-layouts, visit_one(): lax.dynamic_slice_in_dim(arrived_rows, block_index * sub_rows, sub_rows, 0)  61.2 us
    ppermute x11, waiting for transfers between devices, passed_along(): return lax.ppermute(block, axis, route)  47.4 us
    dot_general x6, matrix products, encoder_layer(): jnp.dot(hidden, w_out, preferred_element_type=jnp.float32)  45.1 us
    all_gather x1, waiting for transfers between devices, from_root(): lax.all_gather(x, axis)  41.9 us
    dynamic_slice x48, local copies, waits for them, and re-layouts, attend_block(): lax.dynamic_slice_in_dim(segment_ids, block_start, key_block.shape[0], 0)  36.7 us
    ppermute x11, starting transfers between devices, passed_along(): return lax.ppermute(block, axis, route)  33.6 us
  transfers between devices with their start and end apart: 14, of which 12 were waited for; matrix products, arithmetic and copies ran while one was open for 4% of the time, Pallas kernels for 0%

profile of v1, /device:TPU:231, one launch (start us, length us, event | category | flops | bytes accessed | tf_op | source)
XLA Modules:
  0.0 884.7 jit_solution(16243551358765664413)
XLA Ops:
  8.4 5.8 stack.2
  14.2 9.7 %all-to-all-start = ((bf16[64,18,5248]{2,1,0:T(8,128)(2,1)}), bf16[64,18,5248]{2,1,0:T(8,128)(2,1)}, u32[]{:S(2)}, u32[]{:S(2)}) async-start(bf16[64,18,5248]{2,1,0:T(8,128)(2,1)} %stack.2), calls=%async_computation | async-start | bytes 32243712 | tf_op jit(solution)/shard_map/all_to_all | solution.py:17
  26.8 342.9 %all-to-all-done = bf16[64,18,5248]{2,1,0:T(8,128)(2,1)} async-done(((bf16[64,18,5248]{2,1,0:T(8,128)(2,1)}), bf16[64,18,5248]{2,1,0:T(8,128)(2,1)}, u32[]{:S(2)}, u32[]{:S(2)}) %all-to-all-start) | async-done | bytes 12091424 | tf_op jit(solution)/shard_map/all_to_all | solution.py:17
  369.7 17.1 %reshape.270 = bf16[1152,5248]{1,0:T(8,128)(2,1)} reshape(bf16[64,18,5248]{2,1,0:T(8,128)(2,1)} %all-to-all-done) | data formatting | bytes 24182784 | tf_op jit(solution)/shard_map/reshape | solution.py:18
  386.8 8.4 slice_bitcast_fusion
  395.2 8.4 copy.21
  405.0 134.5 %while.43 = (s32[]{:T(128)}, bf16[243,1152]{1,0:T(8,128)(2,1)S(1)}, bf16[729,1152]{1,0:T(8,128)(2,1)}, pred[]{:T(512)}, bf16[729,1152]{1,0:T(8,128)(2,1)}, /*ind...) while((s32[]{:T(128)}, bf16[243,1152]{1,0:T(8,128)(2,1)S(1)}, ...), condition=%wide.region_3.4_spmd, body=%wide.region_0.3_spmd.sunk | while | flops 2446610432 | bytes 18521884 | solution.py:187
  406.9 7.5 dynamic-slice_select_fusion.4
  421.1 7.8 collective-permute-done
  430.7 7.5 dynamic-slice_select_fusion.4
  445.8 6.9 collective-permute-done
  454.5 7.5 dynamic-slice_select_fusion.4
  469.6 6.1 collective-permute-done
  477.5 7.5 dynamic-slice_select_fusion.4
  492.6 5.2 collective-permute-done
  499.6 7.5 dynamic-slice_select_fusion.4
  520.9 7.5 dynamic-slice_select_fusion.4
  544.4 5.5 reshape.279
  565.9 41.9 %all-gather.6.cloned.1.call-done = bf16[512,1152]{1,0:T(8,128)(2,1)} async-done(((bf16[128,1152]{1,0:T(8,128)(2,1)}), bf16[512,1152]{1,0:T(8,128)(2,1)}) %all-gather.6.cloned.1.call-update) | async-done | bytes 1179664 | tf_op jit(solution)/shard_map/all_gather | solution.py:40
  609.9 12.7 %all_gather.14 = bf16[128,3584]{1,0:T(8,128)(2,1)S(1)} all-gather(bf16[128,896]{1,0:T(8,128)(2,1)S(1)} %fusion.69), channel_id=1, replica_groups=mesh['section'=4,'seq'=64] {'section'}, dimensions={1}, use_global_device_ids=true | all-gather | bytes 1146880 | tf_op jit(solution)/shard_map/all_gather | solution.py:204
  628.6 4.5 collective-permute-start.2
  635.0 70.4 %all-gather.4.cloned.1.call-done = bf16[8192,256]{0,1:T(8,128)(2,1)} async-done(((bf16[128,256]{0,1:T(8,128)(2,1)}), bf16[8192,256]{0,1:T(8,128)(2,1)}) %all-gather.4.cloned.1.call-update) | async-done | bytes 4194320 | tf_op jit(solution)/shard_map/all_gather | solution.py:276
  705.5 158.5 %while.44 = (s32[]{:T(128)}, f32[512]{0:T(512)S(1)}, f32[512]{0:T(512)S(1)}, f32[512,128]{1,0:T(8,128)S(1)}, f32[512]{0:T(512)S(1)}, /*index=5*/f32[512]{0:T(512...) while((s32[]{:T(128)}, f32[512]{0:T(512)S(1)}, ...), condition=%wide.region_15.17_spmd.clone, body=%wide.region_6.16_spmd.clone.sunk | while | flops 69732624 | bytes 3403379 | solution.py:283
  868.0 8.8 collective-permute-done.3
  (971 shorter events, 348.1 us)
Async XLA Ops:
  6.5 616.4 %copy-start = (bf16[3584,128]{1,0:T(8,128)(2,1)S(1)}, bf16[3584,128]{1,0:T(8,128)(2,1)}, u32[]{:S(2)}) copy-start(bf16[3584,128]{1,0:T(8,128)(2,1)} %param.41) | copy-start | bytes 2752516
  14.2 10.0 %copy-start.4 = (s32[64]{0:T(128)S(1)}, s32[64]{0:T(128)}, u32[]{:S(2)}) copy-start(s32[64]{0:T(128)} %param.35) | copy-start | bytes 772
  14.2 10.7 %copy-start.5 = (s32[64]{0:T(128)S(1)}, s32[64]{0:T(128)}, u32[]{:S(2)}) copy-start(s32[64]{0:T(128)} %param.36) | copy-start | bytes 772
  14.2 355.5 %all-to-all-start = ((bf16[64,18,5248]{2,1,0:T(8,128)(2,1)}), bf16[64,18,5248]{2,1,0:T(8,128)(2,1)}, u32[]{:S(2)}, u32[]{:S(2)}) async-start(bf16[64,18,5248]{2,1,0:T(8,128)(2,1)} %stack.2), calls=%async_computation | async-start | bytes 32243712 | tf_op jit(solution)/shard_map/all_to_all | solution.py:17
  23.9 583.8 %all-gather.6.cloned.1.call-start = ((), (), s32[]{:S(2)}) async-start(), calls=%async_computation.2 | async-start | bytes 1474560 | tf_op jit(solution)/shard_map/all_gather | solution.py:40
  403.6 1.4 copy-start.1
  403.6 1.4 copy-start.2
  403.6 1.4 copy-start.3
  414.4 14.5 %collective-permute-start = (bf16[243,1152]{1,0:T(8,128)(2,1)S(1)}, bf16[243,1152]{1,0:T(8,128)(2,1)S(1)}, u32[]{:S(2)}, u32[]{:S(2)}) collective-permute-start(bf16[243,1152]{1,0:T(8,128)(2,1)S(1)} %get-tuple-element.1114), channel_id=1, source_target_pairs={{0,64},{64,128},{128,192},{1,65},{65,129},{129,193},{2,66},{66,130... | collective-permute-start | bytes 1679624 | tf_op jit(solution)/shard_map/while/body/eval_jaxpr/ppermute | solution.py:36
  438.2 14.5 %collective-permute-start = (bf16[243,1152]{1,0:T(8,128)(2,1)S(1)}, bf16[243,1152]{1,0:T(8,128)(2,1)S(1)}, u32[]{:S(2)}, u32[]{:S(2)}) collective-permute-start(bf16[243,1152]{1,0:T(8,128)(2,1)S(1)} %get-tuple-element.1114), channel_id=1, source_target_pairs={{0,64},{64,128},{128,192},{1,65},{65,129},{129,193},{2,66},{66,130... | collective-permute-start | bytes 1679624 | tf_op jit(solution)/shard_map/while/body/eval_jaxpr/ppermute | solution.py:36
  462.0 13.7 %collective-permute-start = (bf16[243,1152]{1,0:T(8,128)(2,1)S(1)}, bf16[243,1152]{1,0:T(8,128)(2,1)S(1)}, u32[]{:S(2)}, u32[]{:S(2)}) collective-permute-start(bf16[243,1152]{1,0:T(8,128)(2,1)S(1)} %get-tuple-element.1114), channel_id=1, source_target_pairs={{0,64},{64,128},{128,192},{1,65},{65,129},{129,193},{2,66},{66,130... | collective-permute-start | bytes 1679624 | tf_op jit(solution)/shard_map/while/body/eval_jaxpr/ppermute | solution.py:36
  485.0 12.8 %collective-permute-start = (bf16[243,1152]{1,0:T(8,128)(2,1)S(1)}, bf16[243,1152]{1,0:T(8,128)(2,1)S(1)}, u32[]{:S(2)}, u32[]{:S(2)}) collective-permute-start(bf16[243,1152]{1,0:T(8,128)(2,1)S(1)} %get-tuple-element.1114), channel_id=1, source_target_pairs={{0,64},{64,128},{128,192},{1,65},{65,129},{129,193},{2,66},{66,130... | collective-permute-start | bytes 1679624 | tf_op jit(solution)/shard_map/while/body/eval_jaxpr/ppermute | solution.py:36
  507.2 11.9 %collective-permute-start = (bf16[243,1152]{1,0:T(8,128)(2,1)S(1)}, bf16[243,1152]{1,0:T(8,128)(2,1)S(1)}, u32[]{:S(2)}, u32[]{:S(2)}) collective-permute-start(bf16[243,1152]{1,0:T(8,128)(2,1)S(1)} %get-tuple-element.1114), channel_id=1, source_target_pairs={{0,64},{64,128},{128,192},{1,65},{65,129},{129,193},{2,66},{66,130... | collective-permute-start | bytes 1679624 | tf_op jit(solution)/shard_map/while/body/eval_jaxpr/ppermute | solution.py:36
  528.4 11.1 %collective-permute-start = (bf16[243,1152]{1,0:T(8,128)(2,1)S(1)}, bf16[243,1152]{1,0:T(8,128)(2,1)S(1)}, u32[]{:S(2)}, u32[]{:S(2)}) collective-permute-start(bf16[243,1152]{1,0:T(8,128)(2,1)S(1)} %get-tuple-element.1114), channel_id=1, source_target_pairs={{0,64},{64,128},{128,192},{1,65},{65,129},{129,193},{2,66},{66,130... | collective-permute-start | bytes 1679624 | tf_op jit(solution)/shard_map/while/body/eval_jaxpr/ppermute | solution.py:36
  555.7 9.1 %collective-permute-start.1 = (bf16[128,1152]{1,0:T(8,128)(2,1)S(1)}, bf16[128,1152]{1,0:T(8,128)(2,1)S(1)}, u32[]{:S(2)}, u32[]{:S(2)}) collective-permute-start(bf16[128,1152]{1,0:T(8,128)(2,1)S(1)} %select_select_fusion), channel_id=1, source_target_pairs={{0,1},{1,2},{2,3},{3,4},{4,5},{5,6},{6,7},{7,8},{8,9},{9,10},{10,1... | collective-permute-start | bytes 884744 | tf_op jit(solution)/shard_map/ppermute | solution.py:36
  565.8 139.6 %all-gather.4.cloned.1.call-start = ((), (), s32[]{:S(2)}) async-start(), calls=%async_computation.1 | async-start | bytes 4259840 | tf_op jit(solution)/shard_map/all_gather | solution.py:276
  607.7 15.2 %copy-start.7 = (f32[3584]{0:T(1024)S(1)}, f32[3584]{0:T(1024)}, u32[]{:S(2)}) copy-start(f32[3584]{0:T(1024)} %param.38) | copy-start | bytes 43012
  609.9 13.6 %copy-start.6 = (bf16[3584,128]{1,0:T(8,128)(2,1)S(1)}, bf16[3584,128]{1,0:T(8,128)(2,1)}, u32[]{:S(2)}) copy-start(bf16[3584,128]{1,0:T(8,128)(2,1)} %param.42) | copy-start | bytes 2752516
  609.9 13.6 %copy-start.9 = (f32[128]{0:T(128)S(1)}, f32[128]{0:T(128)}, u32[]{:S(2)}) copy-start(f32[128]{0:T(128)} %param.43) | copy-start | bytes 1540
  622.9 2.4 copy-start.8
  628.6 6.5 collective-permute-start.2
  864.1 12.8 %collective-permute-start.4 = (f32[512,128]{1,0:T(8,128)S(1)}, f32[512,128]{1,0:T(8,128)S(1)}, u32[]{:S(2)}, u32[]{:S(2)}) collective-permute-start(f32[512,128]{1,0:T(8,128)S(1)} %get-tuple-element.732), channel_id=1, source_target_pairs={{0,32},{1,33},{2,34},{3,35},{4,36},{5,37},{6,38},{7,39},{8,40},{9,... | collective-permute-start | bytes 786440 | tf_op jit(solution)/shard_map/ppermute | solution.py:36
  865.4 11.4 %collective-permute-start.3 = (f32[512]{0:T(512)S(1)}, f32[512]{0:T(512)S(1)}, u32[]{:S(2)}, u32[]{:S(2)}) collective-permute-start(f32[512]{0:T(512)S(1)} %get-tuple-element.731), channel_id=1, source_target_pairs={{0,32},{1,33},{2,34},{3,35},{4,36},{5,37},{6,38},{7,39},{8,40},{9,... | collective-permute-start | bytes 6152 | tf_op jit(solution)/shard_map/ppermute | solution.py:36
  866.7 10.1 %collective-permute-start.5 = (f32[512]{0:T(512)S(1)}, f32[512]{0:T(512)S(1)}, u32[]{:S(2)}, u32[]{:S(2)}) collective-permute-start(f32[512]{0:T(512)S(1)} %get-tuple-element.734), channel_id=1, source_target_pairs={{0,32},{1,33},{2,34},{3,35},{4,36},{5,37},{6,38},{7,39},{8,40},{9,... | collective-permute-start | bytes 6152 | tf_op jit(solution)/shard_map/ppermute | solution.py:36
Sparse Core Ops, SparseCore 0:
  565.9 41.7 all-gather.5
  625.1 80.2 all-gather.3
